TPU v7x, 32 devices: a whole 2x2x4 slice. The times are simulated.
32 devices in a mesh: dp: 2 (over x), tp: 4 (over z), section: 4 (over y, core).
Axes of the slice: x: 2, y: 2, z: 4, core: 2. Of those that a mesh axis runs over, the one named last changes fastest.
Arguments:
- tokens: bfloat16 [256, 2304], P('dp', 'section'), may hold values from -6 to 6
- hidden_grad: bfloat16 [256, 18432], P('dp', ('tp', 'section')), may hold values from -6 to 6
- norm_gain: float32 [2304], replicated, may hold values from 0.5 to 1.5
- w_gate: bfloat16 [2304, 18432], P('dp', ('tp', 'section')), may hold values from -0.125 to 0.125
- w_up: bfloat16 [2304, 18432], P('dp', ('tp', 'section')), may hold values from -0.125 to 0.125
Outputs:
- grad_tokens: bfloat16 [256, 2304], P('dp', ('tp', 'section'))
- grad_gain: float32 [2304], P(('tp', 'section'))
- grad_gate: bfloat16 [2304, 18432], P('dp', ('tp', 'section'))
- grad_up: bfloat16 [2304, 18432], P('dp', ('tp', 'section'))
All inputs are finite; a program needn't handle non-finite values.
Results may differ from a plain program's by a relative error of at most 0.018.
Values may be sent and summed in bfloat16 or wider, within the bound.
A program may use at most 128 MiB of HBM per device.

v0:
```python
import jax
import jax.numpy as jnp
from jax import lax
from jax.sharding import PartitionSpec as P

D = 2304
epsilon = 1e-06


def gated_unit(gate, up):
    return jax.nn.gelu(gate, approximate=True) * up


def shards(tokens, hidden_grad, norm_gain, w_gate, w_up):
    n_dp = lax.axis_size("dp")
    n_model = lax.axis_size(("tp", "section"))
    rows_in = lax.all_gather(tokens, "section", axis=1, tiled=True)
    inputs = rows_in.astype(jnp.float32)
    inv_rms = lax.rsqrt(jnp.mean(inputs * inputs, axis=1) + epsilon)
    normed = (inputs * inv_rms[:, None] * norm_gain).astype(jnp.bfloat16)
    per_device, features = normed.shape
    cols_normed = lax.all_to_all(normed, "dp", split_axis=1, concat_axis=0, tiled=True)
    width = w_gate.shape[1]
    part_gate = jnp.dot(cols_normed, w_gate, preferred_element_type=jnp.float32)
    part_up = jnp.dot(cols_normed, w_up, preferred_element_type=jnp.float32)
    parts = jnp.concatenate([part_gate, part_up], axis=1).astype(jnp.bfloat16)
    parts = lax.all_to_all(parts, "dp", split_axis=0, concat_axis=0, tiled=True)
    sums = jnp.sum(parts.reshape(n_dp, per_device, 2 * width).astype(jnp.float32), axis=0)
    gate, up = (sums[:, :width], sums[:, width:])
    hidden, pull = jax.vjp(gated_unit, gate, up)
    d_both = jnp.concatenate(pull(hidden_grad.astype(jnp.float32)), axis=1).astype(jnp.bfloat16)
    d_all = lax.all_gather(d_both, "dp", axis=0, tiled=True)
    d_gate, d_up = (d_all[:, :width], d_all[:, width:])
    contract_cols = (((1,), (1,)), ((), ()))
    contract_rows = (((0,), (0,)), ((), ()))
    first = lax.dot_general(w_gate, d_gate, contract_cols, preferred_element_type=jnp.float32)
    second = lax.dot_general(w_up, d_up, contract_cols, preferred_element_type=jnp.float32)
    own_width = features // n_model
    per_row = n_model // n_dp
    d_part = (first + second).astype(jnp.bfloat16)
    d_part = d_part.reshape(per_row, own_width, n_dp, per_device).transpose(2, 0, 1, 3)
    d_part = d_part.reshape(n_model * own_width, per_device)
    d_columns = lax.psum_scatter(d_part, ("tp", "section"), scatter_dimension=0, tiled=True)
    moves = [
        (i * n_model + o * per_row + r, o * n_model + i * per_row + r)
        for i in range(n_dp)
        for o in range(n_dp)
        for r in range(per_row)
    ]
    d_columns = lax.ppermute(d_columns, ("dp", "tp", "section"), moves)
    d_normed = d_columns.astype(jnp.float32).T
    offset = lax.axis_index(("tp", "section")) * own_width
    own_inputs = lax.dynamic_slice_in_dim(inputs, offset, own_width, 1)
    own_gain = lax.dynamic_slice_in_dim(norm_gain, offset, own_width, 0)
    gain_part = jnp.sum(d_normed * own_inputs * inv_rms[:, None], axis=0)
    row_part = jnp.sum(own_inputs * own_gain * d_normed, axis=1)
    grad_gain = lax.psum(gain_part, "dp")
    row_sum = lax.psum(row_part, ("tp", "section"))
    grad_tokens = (
        inv_rms[:, None] * own_gain * d_normed
        - own_inputs * (inv_rms**3 * row_sum / features)[:, None]
    )
    grad_gate = lax.dot_general(
        cols_normed, d_gate, contract_rows, preferred_element_type=jnp.float32
    )
    grad_up = lax.dot_general(cols_normed, d_up, contract_rows, preferred_element_type=jnp.float32)
    return (
        grad_tokens.astype(jnp.bfloat16),
        grad_gain,
        grad_gate.astype(jnp.bfloat16),
        grad_up.astype(jnp.bfloat16),
    )


def solution(mesh):
    in_specs = (
        P("dp", "section"),
        P("dp", ("tp", "section")),
        P(),
        P("dp", ("tp", "section")),
        P("dp", ("tp", "section")),
    )
    out_specs = (
        P("dp", ("tp", "section")),
        P(("tp", "section")),
        P("dp", ("tp", "section")),
        P("dp", ("tp", "section")),
    )
    return jax.shard_map(shards, mesh=mesh, in_specs=in_specs, out_specs=out_specs, check_vma=False)
```

profile of v0, /device:TPU:0, one launch (start us, length us, event | category | flops | bytes accessed | tf_op | source)
XLA Modules:
  0.0 196.5 jit_solution(1719906381612836004)
XLA Ops:
  7.2 0.0 copy-start
  7.2 0.0 copy-start.5
  7.2 0.0 all-gather.2.cloned.1.call-start
  7.2 9.4 %all_gather.6 = bf16[128,2304]{0,1:T(8,128)(2,1)S(1)} all-gather(bf16[128,576]{0,1:T(8,128)(2,1)} %param.5), channel_id=1, replica_groups=mesh['dp'=2,'tp'=4,'section'=4] {'section'}, dimensions={1}, use_global_device_ids=true | all-gather | bytes 737280 | tf_op jit(solution)/shard_map/all_gather | solution.py:17
  16.6 0.3 multiply_reduce_fusion
  16.9 0.0 copy-done.5
  16.9 1.2 multiply_convert_fusion
  18.1 2.1 %copy.10 = bf16[128,2,1152]{2,0,1:T(8,128)(2,1)} copy(bf16[128,2,1152]{0,2,1:T(8,128)(2,1)} %bitcast.44) | data formatting | bytes 1179648 | tf_op jit(solution)/shard_map/all_to_all | solution.py:22
  20.3 13.0 %all_to_all.25 = bf16[128,2,1152]{2,0,1:T(8,128)(2,1)S(1)} all-to-all(bf16[128,2,1152]{2,0,1:T(8,128)(2,1)} %copy.10), channel_id=1, replica_groups=mesh['dp'=2,'tp'=4,'section'=4] {'dp'}, dimensions={1} | all-to-all | bytes 1179648 | tf_op jit(solution)/shard_map/all_to_all | solution.py:22
  33.2 0.0 copy-start.1
  33.2 3.0 %fusion.7 = bf16[2,128,1152]{2,1,0:T(8,128)(2,1)S(1)} fusion(bf16[1152,1152]{1,0:T(8,128)(2,1)} %param.9, bf16[128,2,1152]{2,0,1:T(8,128)(2,1)S(1)} %all_to_all.25), kind=kOutput, calls=%fused_computation.8 | convolution fusion | flops 679772160 | bytes 3833856 | tf_op jit(solution)/shard_map/dot_general | solution.py:25
  36.2 0.0 copy-done.1
  36.2 0.0 copy-done
  36.2 1.0 fusion.4
  37.2 0.1 pad_maximum_fusion
  37.3 17.4 %all_to_all.26 = bf16[2,128,2304]{2,1,0:T(8,128)(2,1)S(1)} all-to-all(bf16[2,128,2304]{2,1,0:T(8,128)(2,1)S(1)} %pad_maximum_fusion), channel_id=1, replica_groups=mesh['dp'=2,'tp'=4,'section'=4] {'dp'}, dimensions={0} | all-to-all | bytes 2359296 | tf_op jit(solution)/shard_map/all_to_all | solution.py:27
  54.7 0.0 copy-start.4
  54.7 0.2 convert_reduce_fusion
  54.9 0.8 copy-done.4
  55.7 0.5 fusion.19
  56.2 0.9 pad_maximum_fusion.1
  57.0 0.0 all-gather.2.cloned.1.call-update
  57.0 0.0 reduce-scatter.2.cloned.1.call-start
  57.1 22.7 %all-gather.2.cloned.1.call-done = bf16[256,2304]{1,0:T(8,128)(2,1)} async-done(((bf16[128,2304]{1,0:T(8,128)(2,1)}), bf16[256,2304]{1,0:T(8,128)(2,1)}) %all-gather.2.cloned.1.call-update) | async-done | bytes 1179664 | tf_op jit(solution)/shard_map/all_gather | solution.py:32
  79.8 0.0 copy-start.3
  79.8 0.0 copy-start.6
  79.8 2.2 %fusion.25 = f32[256,1152]{1,0:T(8,128)S(1)} fusion(bf16[1152,1152]{1,0:T(8,128)(2,1)S(1)} %copy-done, bf16[256,2304]{1,0:T(8,128)(2,1)} %all-gather.2.cloned.1.call-done), kind=kOutput, calls=%fused_computation.33 | convolution fusion | flops 679477248 | bytes 4423680 | tf_op jit(solution)/shard_map/dot_general | solution.py:36
  82.1 0.0 copy-done.3
  82.1 0.0 copy-done.6
  82.1 1.9 fusion.11
  84.0 2.1 %copy.11 = bf16[1152,256]{1,0:T(8,128)(2,1)} copy(bf16[1152,256]{0,1:T(8,128)(2,1)} %fusion.11) | data formatting | bytes 1179648 | tf_op jit(solution)/shard_map/convert_element_type | solution.py:40
  86.1 2.5 %reshape.35 = bf16[8,144,2,128]{3,2,1,0:T(2,128)(2,1)} reshape(bf16[1152,256]{1,0:T(8,128)(2,1)} %copy.11) | data formatting | bytes 1179648 | tf_op jit(solution)/shard_map/reshape | solution.py:41
  88.6 2.0 copy.12
  90.5 0.0 reduce-scatter.2.cloned.1.call-update
  90.5 1.1 convert_element_type.31
  91.7 0.1 dynamic_slice.6
  91.7 0.0 copy-start.2
  91.7 3.8 %convolution_convert_fusion.1 = bf16[1152,1152]{1,0:T(8,128)(2,1)} fusion(bf16[256,1152]{1,0:T(8,128)(2,1)} %bitcast.40, bf16[256,2304]{1,0:T(8,128)(2,1)} %all-gather.2.cloned.1.call-done), kind=kOutput, calls=%fused_computation.1 | convolution fusion | flops 680804352 | bytes 3833856 | tf_op jit(solution)/shard_map/dot_general | solution.py:63
  95.5 49.3 %reduce-scatter.2.cloned.1.call-done = bf16[144,128]{1,0:T(8,128)(2,1)} async-done(((bf16[2304,128]{1,0:T(8,128)(2,1)}), bf16[144,128]{1,0:T(8,128)(2,1)}) %reduce-scatter.2.cloned.1.call-update) | async-done | bytes 36880 | tf_op jit(solution)/shard_map/reduce_scatter | solution.py:43
  144.8 1.4 collective-permute-start
  146.2 0.0 copy-done.2
  146.2 3.6 %convolution_convert_fusion = bf16[1152,1152]{1,0:T(8,128)(2,1)} fusion(bf16[256,1152]{1,0:T(8,128)(2,1)S(1)} %bitcast.41, bf16[256,2304]{1,0:T(8,128)(2,1)} %all-gather.2.cloned.1.call-done), kind=kOutput, calls=%fused_computation | convolution fusion | flops 680804352 | bytes 3833856 | tf_op jit(solution)/shard_map/dot_general | solution.py:66
  149.8 0.0 collective-permute-done
  149.8 1.0 fusion.31
  150.8 7.8 %psum.15 = f32[144]{0:T(256)} all-reduce(f32[144]{0:T(256)S(1)} %get-tuple-element.4), channel_id=1, replica_groups=mesh['dp'=2,'tp'=4,'section'=4] {'dp'}, use_global_device_ids=true, to_apply=%region_6.0 | all-reduce | flops 144 | bytes 1152 | tf_op jit(solution)/shard_map/psum | solution.py:57
  158.6 29.5 %psum.14 = f32[128]{0:T(128)S(1)} all-reduce(f32[128]{0:T(128)S(1)} %get-tuple-element.5), channel_id=1, replica_groups=mesh['dp'=2,'tp'=4,'section'=4] {'tp','section'}, use_global_device_ids=true, to_apply=%region_4.0 | all-reduce | flops 128 | bytes 1024 | tf_op jit(solution)/shard_map/psum | solution.py:58
  188.1 1.6 fusion.28
  (2 shorter events, 0.0 us)
Async XLA Ops:
  7.2 29.0 %copy-start = (bf16[1152,1152]{1,0:T(8,128)(2,1)S(1)}, bf16[1152,1152]{1,0:T(8,128)(2,1)}, u32[]{:S(2)}) copy-start(bf16[1152,1152]{1,0:T(8,128)(2,1)} %param.8) | copy-start | bytes 7962628
  7.2 9.8 %copy-start.5 = (f32[2304]{0:T(1024)S(1)}, f32[2304]{0:T(1024)}, u32[]{:S(2)}) copy-start(f32[2304]{0:T(1024)} %param.7) | copy-start | bytes 27652
  7.2 72.6 %all-gather.2.cloned.1.call-start = ((), (), s32[]{:S(2)}) async-start(), calls=%async_computation.3 | async-start | bytes 1769472 | tf_op jit(solution)/shard_map/all_gather | solution.py:32
  33.2 3.0 %copy-start.1 = (bf16[128,2,1152]{2,0,1:T(8,128)(2,1)}, bf16[128,2,1152]{2,0,1:T(8,128)(2,1)S(1)}, u32[]{:S(2)}) copy-start(bf16[128,2,1152]{2,0,1:T(8,128)(2,1)S(1)} %all_to_all.25) | copy-start | bytes 1769476
  54.7 1.0 copy-start.4
  57.0 87.8 %reduce-scatter.2.cloned.1.call-start = ((), (), s32[]{:S(2)}) async-start(), calls=%async_computation.4 | async-start | bytes 626688 | tf_op jit(solution)/shard_map/reduce_scatter | solution.py:43
  79.8 2.3 %copy-start.3 = (bf16[256,2304]{1,0:T(8,128)(2,1)S(1)}, bf16[256,2304]{1,0:T(8,128)(2,1)}, u32[]{:S(2)}) copy-start(bf16[256,2304]{1,0:T(8,128)(2,1)} %all-gather.2.cloned.1.call-done) | copy-start | bytes 3538948
  79.8 2.3 %copy-start.6 = (bf16[1152,1152]{1,0:T(8,128)(2,1)S(1)}, bf16[1152,1152]{1,0:T(8,128)(2,1)}, u32[]{:S(2)}) copy-start(bf16[1152,1152]{1,0:T(8,128)(2,1)} %param.9) | copy-start | bytes 7962628
  91.7 54.5 %copy-start.2 = (bf16[128,2,1152]{2,0,1:T(8,128)(2,1)S(1)}, bf16[128,2,1152]{2,0,1:T(8,128)(2,1)}, u32[]{:S(2)}) copy-start(bf16[128,2,1152]{2,0,1:T(8,128)(2,1)} %copy-done.1) | copy-start | bytes 1769476
  144.8 5.0 %collective-permute-start = (bf16[144,128]{1,0:T(8,128)(2,1)}, bf16[144,128]{1,0:T(8,128)(2,1)S(1)}, u32[]{:S(2)}, u32[]{:S(2)}) collective-permute-start(bf16[144,128]{1,0:T(8,128)(2,1)} %reduce-scatter.2.cloned.1.call-done), channel_id=1, source_target_pairs={{0,0},{1,1},{2,2},{3,3},{4,4},{5,5},{6,6},{7,7},{8,16},{9,17},{10,... | collective-permute-start | bytes 110600 | tf_op jit(solution)/shard_map/ppermute | solution.py:50
Sparse Core Ops, SparseCore 0:
  57.2 22.6 all-gather.1
  90.7 54.0 reduce-scatter.1
where the time goes:
time: 197 us
  blocking collectives  77 us (39%)
  waiting for transfers between devices  72 us (37%)
  matrix products  15.4 us (8%)
  between operations  14.1 us (7%)
  local copies, waits for them, and re-layouts  9.56 us (5%)
  other arithmetic  6.9 us (4%)
    reduce_scatter x1, waiting for transfers between devices, shards(): lax.psum_scatter(d_part, ('tp', 'section'), scatter_dimension=0, tiled=True)  49.3 us
    psum x1, blocking collectives, shards(): row_sum = lax.psum(row_part, ('tp', 'section'))  29.5 us
    all_gather x1, waiting for transfers between devices, shards(): d_all = lax.all_gather(d_both, 'dp', axis=0, tiled=True)  22.7 us
    all_to_all x1, blocking collectives, shards(): parts = lax.all_to_all(parts, 'dp', split_axis=0, concat_axis=0, tiled=True)  17.4 us
    all_to_all x1, blocking collectives, shards(): lax.all_to_all(normed, 'dp', split_axis=1, concat_axis=0, tiled=True)  13 us
    all_gather x1, blocking collectives, shards(): rows_in = lax.all_gather(tokens, 'section', axis=1, tiled=True)  9.38 us
    psum x1, blocking collectives, shards(): grad_gain = lax.psum(gain_part, 'dp')  7.8 us
  transfers between devices with their start and end apart: 3, of which 2 were waited for; matrix products, arithmetic and copies ran while one was open for 4% of the time, Pallas kernels for 0%

commit v1 on v0

--- a/solution.py
+++ b/solution.py
@@ -55,7 +55,7 @@
     gain_part = jnp.sum(d_normed * own_inputs * inv_rms[:, None], axis=0)
     row_part = jnp.sum(own_inputs * own_gain * d_normed, axis=1)
     grad_gain = lax.psum(gain_part, "dp")
-    row_sum = lax.psum(row_part, ("tp", "section"))
+    row_sum = jnp.sum(lax.all_gather(row_part, ("tp", "section")), axis=0)
     grad_tokens = (
         inv_rms[:, None] * own_gain * d_normed
         - own_inputs * (inv_rms**3 * row_sum / features)[:, None]

time: 197 us -> 189 us (0.959)
  blocking collectives: 77 us -> 68.4 us
    psum x1 -> x0, blocking collectives: 29.5 us -> none  [shards(): row_sum = lax.psum(row_part, ('tp', 'section'))]
    all_gather x0 -> x1, blocking collectives: none -> 20.9 us  [shards(): row_sum = jnp.sum(lax.all_gather(row_part, ('tp', 'section')), axis=0)]
  transfers between devices with their start and end apart: 3 -> 3, of which waited for: 2 -> 2; matrix products, arithmetic and copies ran while one was open for 4% -> 5% of each run, Pallas kernels for 0% -> 0%
where the time goes in v1:
time: 189 us; the launch traced here: 188 us
  waiting for transfers between devices  72 us (38%)
  blocking collectives  68.4 us (36%)
  matrix products  15.4 us (8%)
  between operations  14.1 us (7%)
  local copies, waits for them, and re-layouts  9.56 us (5%)
  other arithmetic  6.93 us (4%)
    reduce_scatter x1, waiting for transfers between devices, shards(): lax.psum_scatter(d_part, ('tp', 'section'), scatter_dimension=0, tiled=True)  49.3 us
    all_gather x1, waiting for transfers between devices, shards(): d_all = lax.all_gather(d_both, 'dp', axis=0, tiled=True)  22.7 us
    all_gather x1, blocking collectives, shards(): row_sum = jnp.sum(lax.all_gather(row_part, ('tp', 'section')), axis=0)  20.9 us
    all_to_all x1, blocking collectives, shards(): parts = lax.all_to_all(parts, 'dp', split_axis=0, concat_axis=0, tiled=True)  17.4 us
    all_to_all x1, blocking collectives, shards(): lax.all_to_all(normed, 'dp', split_axis=1, concat_axis=0, tiled=True)  13 us
    all_gather x1, blocking collectives, shards(): rows_in = lax.all_gather(tokens, 'section', axis=1, tiled=True)  9.38 us
    psum x1, blocking collectives, shards(): grad_gain = lax.psum(gain_part, 'dp')  7.8 us
    dot_general x1, matrix products, shards(): lax.dot_general(cols_normed, d_gate, contract_rows, preferred_element_typ...  3.79 us
  transfers between devices with their start and end apart: 3, of which 2 were waited for; matrix products, arithmetic and copies ran while one was open for 5% of the time, Pallas kernels for 0%

profile of v1, /device:TPU:0, one launch (start us, length us, event | category | flops | bytes accessed | tf_op | source)
XLA Modules:
  0.0 187.9 jit_solution(10869562676785284383)
XLA Ops:
  7.2 0.0 copy-start
  7.2 0.0 copy-start.5
  7.2 0.0 all-gather.4.cloned.1.call-start
  7.2 9.4 %all_gather.12 = bf16[128,2304]{0,1:T(8,128)(2,1)S(1)} all-gather(bf16[128,576]{0,1:T(8,128)(2,1)} %param.5), channel_id=1, replica_groups=mesh['dp'=2,'tp'=4,'section'=4] {'section'}, dimensions={1}, use_global_device_ids=true | all-gather | bytes 737280 | tf_op jit(solution)/shard_map/all_gather | solution.py:17
  16.6 0.3 multiply_reduce_fusion
  16.9 0.0 copy-done.5
  16.9 1.2 multiply_convert_fusion
  18.1 2.1 %copy.13 = bf16[128,2,1152]{2,0,1:T(8,128)(2,1)} copy(bf16[128,2,1152]{0,2,1:T(8,128)(2,1)} %bitcast.45) | data formatting | bytes 1179648 | tf_op jit(solution)/shard_map/all_to_all | solution.py:22
  20.3 13.0 %all_to_all.25 = bf16[128,2,1152]{2,0,1:T(8,128)(2,1)S(1)} all-to-all(bf16[128,2,1152]{2,0,1:T(8,128)(2,1)} %copy.13), channel_id=1, replica_groups=mesh['dp'=2,'tp'=4,'section'=4] {'dp'}, dimensions={1} | all-to-all | bytes 1179648 | tf_op jit(solution)/shard_map/all_to_all | solution.py:22
  33.2 0.0 copy-start.1
  33.2 3.0 %fusion.7 = bf16[2,128,1152]{2,1,0:T(8,128)(2,1)S(1)} fusion(bf16[1152,1152]{1,0:T(8,128)(2,1)} %param.9, bf16[128,2,1152]{2,0,1:T(8,128)(2,1)S(1)} %all_to_all.25), kind=kOutput, calls=%fused_computation.8 | convolution fusion | flops 679772160 | bytes 3833856 | tf_op jit(solution)/shard_map/dot_general | solution.py:25
  36.2 0.0 copy-done.1
  36.2 0.0 copy-done
  36.2 1.0 fusion.4
  37.2 0.1 pad_maximum_fusion
  37.3 17.4 %all_to_all.26 = bf16[2,128,2304]{2,1,0:T(8,128)(2,1)S(1)} all-to-all(bf16[2,128,2304]{2,1,0:T(8,128)(2,1)S(1)} %pad_maximum_fusion), channel_id=1, replica_groups=mesh['dp'=2,'tp'=4,'section'=4] {'dp'}, dimensions={0} | all-to-all | bytes 2359296 | tf_op jit(solution)/shard_map/all_to_all | solution.py:27
  54.7 0.0 copy-start.4
  54.7 0.2 convert_reduce_fusion
  54.9 0.8 copy-done.4
  55.7 0.5 fusion.19
  56.2 0.9 pad_maximum_fusion.1
  57.0 0.0 all-gather.4.cloned.1.call-update
  57.0 0.0 reduce-scatter.2.cloned.1.call-start
  57.1 22.7 %all-gather.4.cloned.1.call-done = bf16[256,2304]{1,0:T(8,128)(2,1)} async-done(((bf16[128,2304]{1,0:T(8,128)(2,1)}), bf16[256,2304]{1,0:T(8,128)(2,1)}) %all-gather.4.cloned.1.call-update) | async-done | bytes 1179664 | tf_op jit(solution)/shard_map/all_gather | solution.py:32
  79.8 0.0 copy-start.3
  79.8 0.0 copy-start.6
  79.8 2.2 %fusion.25 = f32[256,1152]{1,0:T(8,128)S(1)} fusion(bf16[1152,1152]{1,0:T(8,128)(2,1)S(1)} %copy-done, bf16[256,2304]{1,0:T(8,128)(2,1)} %all-gather.4.cloned.1.call-done), kind=kOutput, calls=%fused_computation.33 | convolution fusion | flops 679477248 | bytes 4423680 | tf_op jit(solution)/shard_map/dot_general | solution.py:36
  82.1 0.0 copy-done.3
  82.1 0.0 copy-done.6
  82.1 1.9 fusion.11
  84.0 2.1 %copy.14 = bf16[1152,256]{1,0:T(8,128)(2,1)} copy(bf16[1152,256]{0,1:T(8,128)(2,1)} %fusion.11) | data formatting | bytes 1179648 | tf_op jit(solution)/shard_map/convert_element_type | solution.py:40
  86.1 2.5 %reshape.42 = bf16[8,144,2,128]{3,2,1,0:T(2,128)(2,1)} reshape(bf16[1152,256]{1,0:T(8,128)(2,1)} %copy.14) | data formatting | bytes 1179648 | tf_op jit(solution)/shard_map/reshape | solution.py:41
  88.6 2.0 %copy.15 = bf16[2,8,144,128]{3,2,1,0:T(8,128)(2,1)} copy(bf16[2,8,144,128]{3,0,2,1:T(2,128)(2,1)} %bitcast.44) | data formatting | bytes 1179648 | tf_op jit(solution)/shard_map/transpose | solution.py:41
  90.5 0.0 reduce-scatter.2.cloned.1.call-update
  90.5 1.1 convert_element_type.31
  91.7 0.1 dynamic_slice.6
  91.7 0.0 copy-start.2
  91.7 3.8 %convolution_convert_fusion.1 = bf16[1152,1152]{1,0:T(8,128)(2,1)} fusion(bf16[256,1152]{1,0:T(8,128)(2,1)} %bitcast.41, bf16[256,2304]{1,0:T(8,128)(2,1)} %all-gather.4.cloned.1.call-done), kind=kOutput, calls=%fused_computation.1 | convolution fusion | flops 680804352 | bytes 3833856 | tf_op jit(solution)/shard_map/dot_general | solution.py:63
  95.5 49.3 %reduce-scatter.2.cloned.1.call-done = bf16[144,128]{1,0:T(8,128)(2,1)} async-done(((bf16[2304,128]{1,0:T(8,128)(2,1)}), bf16[144,128]{1,0:T(8,128)(2,1)}) %reduce-scatter.2.cloned.1.call-update) | async-done | bytes 36880 | tf_op jit(solution)/shard_map/reduce_scatter | solution.py:43
  144.8 1.4 collective-permute-start
  146.2 0.0 copy-done.2
  146.2 3.6 %convolution_convert_fusion = bf16[1152,1152]{1,0:T(8,128)(2,1)} fusion(bf16[256,1152]{1,0:T(8,128)(2,1)S(1)} %bitcast.42, bf16[256,2304]{1,0:T(8,128)(2,1)} %all-gather.4.cloned.1.call-done), kind=kOutput, calls=%fused_computation | convolution fusion | flops 680804352 | bytes 3833856 | tf_op jit(solution)/shard_map/dot_general | solution.py:66
  149.8 0.0 collective-permute-done
  149.8 1.0 fusion.31
  150.8 7.8 %psum.7 = f32[144]{0:T(256)} all-reduce(f32[144]{0:T(256)S(1)} %get-tuple-element.4), channel_id=1, replica_groups=mesh['dp'=2,'tp'=4,'section'=4] {'dp'}, use_global_device_ids=true, to_apply=%region_6.0 | all-reduce | flops 144 | bytes 1152 | tf_op jit(solution)/shard_map/psum | solution.py:57
  158.6 20.9 %all-gather.1 = f32[16,1,128]{2,1,0:T(1,128)S(1)} all-gather(f32[1,1,128]{2,1,0:T(1,128)S(1)} %bitcast.46), channel_id=2, replica_groups=mesh['dp'=2,'tp'=4,'section'=4] {'tp','section'}, dimensions={0}, use_global_device_ids=true | all-gather | bytes 8704 | tf_op jit(solution)/shard_map/all_gather | solution.py:58
  179.5 1.6 fusion.28
  (3 shorter events, 0.1 us)
Async XLA Ops:
  7.2 29.0 %copy-start = (bf16[1152,1152]{1,0:T(8,128)(2,1)S(1)}, bf16[1152,1152]{1,0:T(8,128)(2,1)}, u32[]{:S(2)}) copy-start(bf16[1152,1152]{1,0:T(8,128)(2,1)} %param.8) | copy-start | bytes 7962628
  7.2 9.8 %copy-start.5 = (f32[2304]{0:T(1024)S(1)}, f32[2304]{0:T(1024)}, u32[]{:S(2)}) copy-start(f32[2304]{0:T(1024)} %param.7) | copy-start | bytes 27652
  7.2 72.6 %all-gather.4.cloned.1.call-start = ((), (), s32[]{:S(2)}) async-start(), calls=%async_computation.3 | async-start | bytes 1769472 | tf_op jit(solution)/shard_map/all_gather | solution.py:32
  33.2 3.0 %copy-start.1 = (bf16[128,2,1152]{2,0,1:T(8,128)(2,1)}, bf16[128,2,1152]{2,0,1:T(8,128)(2,1)S(1)}, u32[]{:S(2)}) copy-start(bf16[128,2,1152]{2,0,1:T(8,128)(2,1)S(1)} %all_to_all.25) | copy-start | bytes 1769476
  54.7 1.0 copy-start.4
  57.0 87.8 %reduce-scatter.2.cloned.1.call-start = ((), (), s32[]{:S(2)}) async-start(), calls=%async_computation.4 | async-start | bytes 626688 | tf_op jit(solution)/shard_map/reduce_scatter | solution.py:43
  79.8 2.3 %copy-start.3 = (bf16[256,2304]{1,0:T(8,128)(2,1)S(1)}, bf16[256,2304]{1,0:T(8,128)(2,1)}, u32[]{:S(2)}) copy-start(bf16[256,2304]{1,0:T(8,128)(2,1)} %all-gather.4.cloned.1.call-done) | copy-start | bytes 3538948
  79.8 2.3 %copy-start.6 = (bf16[1152,1152]{1,0:T(8,128)(2,1)S(1)}, bf16[1152,1152]{1,0:T(8,128)(2,1)}, u32[]{:S(2)}) copy-start(bf16[1152,1152]{1,0:T(8,128)(2,1)} %param.9) | copy-start | bytes 7962628
  91.7 54.5 %copy-start.2 = (bf16[128,2,1152]{2,0,1:T(8,128)(2,1)S(1)}, bf16[128,2,1152]{2,0,1:T(8,128)(2,1)}, u32[]{:S(2)}) copy-start(bf16[128,2,1152]{2,0,1:T(8,128)(2,1)} %copy-done.1) | copy-start | bytes 1769476
  144.8 5.0 %collective-permute-start = (bf16[144,128]{1,0:T(8,128)(2,1)}, bf16[144,128]{1,0:T(8,128)(2,1)S(1)}, u32[]{:S(2)}, u32[]{:S(2)}) collective-permute-start(bf16[144,128]{1,0:T(8,128)(2,1)} %reduce-scatter.2.cloned.1.call-done), channel_id=1, source_target_pairs={{0,0},{1,1},{2,2},{3,3},{4,4},{5,5},{6,6},{7,7},{8,16},{9,17},{10,... | collective-permute-start | bytes 110600 | tf_op jit(solution)/shard_map/ppermute | solution.py:50
Sparse Core Ops, SparseCore 0:
  57.2 22.6 all-gather.3
  90.7 54.0 reduce-scatter.1
